TPU v7x, 32 devices: a whole 2x2x4 slice. The times are simulated.
32 devices in a mesh: bank: 8 (over y, x, core), lane: 4 (over z).
Axes of the slice: x: 2, y: 2, z: 4, core: 2. Of those that a mesh axis runs over, the one named last changes fastest.
Arguments:
- amplitudes: float32 [2, 128, 128, 128], P(None, ('bank', 'lane')), may hold values from -6 to 6
- energies: float32 [128, 128, 128], P(('bank', 'lane')), may hold values from -2 to 2
- phase_angles: float32 [2, 128], replicated, may hold values from 0.3 to 1.2
- mix_angles: float32 [2, 4], replicated, may hold values from 0.3 to 1.2
Outputs:
- final_parts: float32 [2, 128, 128, 128], P(None, ('bank', 'lane'))
- marginal: float32 [16, 128, 128], P('lane', 'bank')
All inputs are finite; a program needn't handle non-finite values.
Results may differ from a plain program's by a relative error of at most 0.0003.
Values sent between devices are 32-bit elements; how exact they have to be, the bound alone decides.
A program may use at most 64 MiB of HBM per device.

v0:
```python
import jax
import jax.numpy as jnp
from jax import lax
from jax.sharding import PartitionSpec as P

LAYERS = 2


def count_bits(values, count):
    places = jnp.arange(count.bit_length() - 1, dtype=jnp.int32)
    return jnp.sum(values[..., None] >> places & 1, axis=-1)


def turn_table(count, angle):
    rank = jnp.arange(count, dtype=jnp.int32)
    apart = count_bits(rank[:, None] ^ rank[None, :], count)
    bits = count.bit_length() - 1
    size = jnp.cos(angle) ** (bits - apart).astype(jnp.float32) * jnp.sin(angle) ** apart.astype(
        jnp.float32
    )
    real_sign = jnp.where(apart % 4 == 0, 1.0, jnp.where(apart % 4 == 2, -1.0, 0.0)).astype(
        jnp.float32
    )
    imag_sign = jnp.where(apart % 4 == 1, -1.0, jnp.where(apart % 4 == 3, 1.0, 0.0)).astype(
        jnp.float32
    )
    return (size * real_sign, size * imag_sign)


def apply_along(values, dim, angle):
    real_part, imag_part = turn_table(values.shape[dim], angle)

    def times(table):
        moved = jnp.tensordot(values, table, axes=([dim], [0]), precision=lax.Precision.HIGHEST)
        return jnp.moveaxis(moved, -1, dim)

    by_real = times(real_part)
    by_imag = times(imag_part)
    return jnp.stack([by_real[0] - by_imag[1], by_real[1] + by_imag[0]])


def diagonal_step(values, levels, angle):
    turn = angle * levels
    return jnp.stack(
        [
            values[0] * jnp.cos(turn) + values[1] * jnp.sin(turn),
            values[1] * jnp.cos(turn) - values[0] * jnp.sin(turn),
        ]
    )


def on_device(amplitudes, energies, phase_angles, mix_angles):
    values = amplitudes
    for layer in range(LAYERS):
        values = diagonal_step(values, energies, phase_angles[layer])
        values = apply_along(values, 3, mix_angles[layer, 0])
        values = apply_along(values, 2, mix_angles[layer, 1])
        moved = lax.all_to_all(values, "bank", split_axis=2, concat_axis=1, tiled=True)
        moved = apply_along(moved, 1, mix_angles[layer, 2])
        values = lax.all_to_all(moved, "bank", split_axis=1, concat_axis=2, tiled=True)
        moved = lax.all_to_all(values, "lane", split_axis=3, concat_axis=1, tiled=True)
        spread = moved.reshape(2, lax.axis_size("lane"), -1, moved.shape[2], moved.shape[3])
        moved = apply_along(spread, 1, mix_angles[layer, 3]).reshape(moved.shape)
        values = lax.all_to_all(moved, "lane", split_axis=1, concat_axis=3, tiled=True)
    chance = values[0] * values[0] + values[1] * values[1]
    marginal = lax.psum_scatter(chance, "bank", scatter_dimension=1, tiled=True) / lax.axis_size(
        "bank"
    )
    return (values, marginal)


def solution(mesh):
    placed = (P(None, ("bank", "lane"), None, None), P(("bank", "lane"), None, None), P(), P())
    return jax.shard_map(
        on_device,
        mesh=mesh,
        in_specs=placed,
        out_specs=(P(None, ("bank", "lane"), None, None), P("lane", "bank", None)),
        check_vma=False,
    )
```

profile of v0, /device:TPU:0, one launch (start us, length us, event | category | flops | bytes accessed | tf_op | source)
XLA Modules:
  0.0 223.7 jit_solution(4671469216967505596)
XLA Ops:
  7.2 1.7 fusion.221
  10.9 2.0 fusion.14
  16.1 1.1 convolution_bitcast_fusion.11
  17.2 1.1 convolution_bitcast_fusion.10
  18.4 1.0 copy.120
  19.4 5.2 %all-to-all-start = ((f32[2,4,128,128]{3,1,0,2:T(4,128)}), f32[2,4,128,128]{3,1,0,2:T(4,128)S(1)}, u32[]{:S(2)}, u32[]{:S(2)}) async-start(f32[2,4,128,128]{3,1,0,2:T(4,128)} %copy.120), calls=%async_computation | async-start | bytes 1048576 | tf_op jit(solution)/shard_map/all_to_all | solution.py:58
  26.0 8.3 %all-to-all-done = f32[2,4,128,128]{3,1,0,2:T(4,128)S(1)} async-done(((f32[2,4,128,128]{3,1,0,2:T(4,128)}), f32[2,4,128,128]{3,1,0,2:T(4,128)S(1)}, u32[]{:S(2)}, u32[]{:S(2)}) %all-to-all-start) | async-done | bytes 524320 | tf_op jit(solution)/shard_map/all_to_all | solution.py:58
  36.6 12.1 %all_to_all.135 = f32[2,32,16,128]{3,2,0,1:T(8,128)S(1)} all-to-all(f32[2,32,16,128]{3,2,0,1:T(8,128)S(1)} %copy.125), channel_id=1, replica_groups=mesh['bank'=8,'lane'=4] {'bank'}, dimensions={1} | all-to-all | bytes 1048576 | tf_op jit(solution)/shard_map/all_to_all | solution.py:60
  48.7 1.0 copy.128
  49.7 4.9 %all-to-all-start.2 = ((f32[2,4,128,128]{2,1,0,3:T(4,128)}), f32[2,4,128,128]{2,1,0,3:T(4,128)S(1)}, u32[]{:S(2)}, u32[]{:S(2)}) async-start(f32[2,4,128,128]{2,1,0,3:T(4,128)} %copy.128), calls=%async_computation.2 | async-start | bytes 1048576 | tf_op jit(solution)/shard_map/all_to_all | solution.py:61
  56.1 12.5 %all-to-all-done.2 = f32[2,4,128,128]{2,1,0,3:T(4,128)S(1)} async-done(((f32[2,4,128,128]{2,1,0,3:T(4,128)}), f32[2,4,128,128]{2,1,0,3:T(4,128)S(1)}, u32[]{:S(2)}, u32[]{:S(2)}) %all-to-all-start.2) | async-done | bytes 524320 | tf_op jit(solution)/shard_map/all_to_all | solution.py:61
  68.5 1.3 convolution_bitcast_fusion.7
  69.9 1.3 convolution_bitcast_fusion.6
  71.5 0.8 copy.135
  72.3 3.7 %all-to-all-start.3 = ((f32[2,16,128,32]{2,3,0,1:T(8,128)}), f32[2,16,128,32]{2,3,0,1:T(8,128)S(1)}, u32[]{:S(2)}, u32[]{:S(2)}) async-start(f32[2,16,128,32]{2,3,0,1:T(8,128)} %copy.135), calls=%async_computation.3 | async-start | bytes 1048576 | tf_op jit(solution)/shard_map/all_to_all | solution.py:64
  78.6 11.2 %all-to-all-done.3 = f32[2,16,128,32]{2,3,0,1:T(8,128)S(1)} async-done(((f32[2,16,128,32]{2,3,0,1:T(8,128)}), f32[2,16,128,32]{2,3,0,1:T(8,128)S(1)}, u32[]{:S(2)}, u32[]{:S(2)}) %all-to-all-start.3) | async-done | bytes 524320 | tf_op jit(solution)/shard_map/all_to_all | solution.py:64
  91.0 1.0 add_bitcast_fusion
  93.7 1.1 convolution_bitcast_fusion.5
  94.8 1.1 convolution_bitcast_fusion.4
  96.0 1.0 copy.145
  97.0 3.5 %all-to-all-start.4 = ((f32[2,4,128,128]{3,1,0,2:T(4,128)}), f32[2,4,128,128]{3,1,0,2:T(4,128)S(1)}, u32[]{:S(2)}, u32[]{:S(2)}) async-start(f32[2,4,128,128]{3,1,0,2:T(4,128)} %copy.145), calls=%async_computation.4 | async-start | bytes 1048576 | tf_op jit(solution)/shard_map/all_to_all | solution.py:58
  102.0 8.1 %all-to-all-done.4 = f32[2,4,128,128]{3,1,0,2:T(4,128)S(1)} async-done(((f32[2,4,128,128]{3,1,0,2:T(4,128)}), f32[2,4,128,128]{3,1,0,2:T(4,128)S(1)}, u32[]{:S(2)}, u32[]{:S(2)}) %all-to-all-start.4) | async-done | bytes 524320 | tf_op jit(solution)/shard_map/all_to_all | solution.py:58
  112.4 12.1 %all_to_all.136 = f32[2,32,16,128]{3,2,0,1:T(8,128)S(1)} all-to-all(f32[2,32,16,128]{3,2,0,1:T(8,128)S(1)} %copy.150), channel_id=1, replica_groups=mesh['bank'=8,'lane'=4] {'bank'}, dimensions={1} | all-to-all | bytes 1048576 | tf_op jit(solution)/shard_map/all_to_all | solution.py:60
  124.6 1.0 copy.153
  125.6 3.5 %all-to-all-start.6 = ((f32[2,4,128,128]{2,1,0,3:T(4,128)}), f32[2,4,128,128]{2,1,0,3:T(4,128)S(1)}, u32[]{:S(2)}, u32[]{:S(2)}) async-start(f32[2,4,128,128]{2,1,0,3:T(4,128)} %copy.153), calls=%async_computation.6 | async-start | bytes 1048576 | tf_op jit(solution)/shard_map/all_to_all | solution.py:61
  130.5 12.7 %all-to-all-done.6 = f32[2,4,128,128]{2,1,0,3:T(4,128)S(1)} async-done(((f32[2,4,128,128]{2,1,0,3:T(4,128)}), f32[2,4,128,128]{2,1,0,3:T(4,128)S(1)}, u32[]{:S(2)}, u32[]{:S(2)}) %all-to-all-start.6) | async-done | bytes 524320 | tf_op jit(solution)/shard_map/all_to_all | solution.py:61
  143.2 1.3 convolution_bitcast_fusion.1
  144.6 1.3 convolution_bitcast_fusion
  146.2 16.4 %all_to_all.137 = f32[2,16,128,32]{2,3,0,1:T(8,128)S(1)} all-to-all(f32[2,16,128,32]{2,3,0,1:T(8,128)S(1)} %copy.160), channel_id=1, replica_groups=mesh['bank'=8,'lane'=4] {'lane'}, dimensions={1} | all-to-all | bytes 1048576 | tf_op jit(solution)/shard_map/all_to_all | solution.py:64
  162.8 0.8 copy.164
  165.6 1.0 copy.165
  166.6 48.9 %all-reduce.3.cloned.1.call-done = f32[4,128,128]{2,0,1:T(4,128)} async-done(((f32[4,128,128]{2,0,1:T(4,128)}), f32[4,128,128]{2,0,1:T(4,128)}) %all-reduce.3.cloned.1.call-update) | async-done | bytes 262160
  (65 shorter events, 13.1 us)
Async XLA Ops:
  10.2 0.7 copy-start.1
  19.4 14.9 %all-to-all-start = ((f32[2,4,128,128]{3,1,0,2:T(4,128)}), f32[2,4,128,128]{3,1,0,2:T(4,128)S(1)}, u32[]{:S(2)}, u32[]{:S(2)}) async-start(f32[2,4,128,128]{3,1,0,2:T(4,128)} %copy.120), calls=%async_computation | async-start | bytes 1048576 | tf_op jit(solution)/shard_map/all_to_all | solution.py:58
  49.7 18.8 %all-to-all-start.2 = ((f32[2,4,128,128]{2,1,0,3:T(4,128)}), f32[2,4,128,128]{2,1,0,3:T(4,128)S(1)}, u32[]{:S(2)}, u32[]{:S(2)}) async-start(f32[2,4,128,128]{2,1,0,3:T(4,128)} %copy.128), calls=%async_computation.2 | async-start | bytes 1048576 | tf_op jit(solution)/shard_map/all_to_all | solution.py:61
  72.3 17.5 %all-to-all-start.3 = ((f32[2,16,128,32]{2,3,0,1:T(8,128)}), f32[2,16,128,32]{2,3,0,1:T(8,128)S(1)}, u32[]{:S(2)}, u32[]{:S(2)}) async-start(f32[2,16,128,32]{2,3,0,1:T(8,128)} %copy.135), calls=%async_computation.3 | async-start | bytes 1048576 | tf_op jit(solution)/shard_map/all_to_all | solution.py:64
  90.1 1.0 copy-start
  97.0 13.2 %all-to-all-start.4 = ((f32[2,4,128,128]{3,1,0,2:T(4,128)}), f32[2,4,128,128]{3,1,0,2:T(4,128)S(1)}, u32[]{:S(2)}, u32[]{:S(2)}) async-start(f32[2,4,128,128]{3,1,0,2:T(4,128)} %copy.145), calls=%async_computation.4 | async-start | bytes 1048576 | tf_op jit(solution)/shard_map/all_to_all | solution.py:58
  125.6 17.7 %all-to-all-start.6 = ((f32[2,4,128,128]{2,1,0,3:T(4,128)}), f32[2,4,128,128]{2,1,0,3:T(4,128)S(1)}, u32[]{:S(2)}, u32[]{:S(2)}) async-start(f32[2,4,128,128]{2,1,0,3:T(4,128)} %copy.153), calls=%async_computation.6 | async-start | bytes 1048576 | tf_op jit(solution)/shard_map/all_to_all | solution.py:61
  129.1 86.4 %all-reduce.3.cloned.1.call-start = ((), (), s32[]{:S(2)}) async-start(), calls=%async_computation.8 | async-start | bytes 524288
  163.6 0.7 copy-start.2
Sparse Core Ops, SparseCore 0:
  163.7 51.6 all-reduce.2
where the time goes:
time: 225 us; the launch traced here: 224 us
  waiting for transfers between devices  102 us (45%)
  blocking collectives  40.7 us (18%)
  between operations  26.5 us (12%)
  starting transfers between devices  20.7 us (9%)
  matrix products  15.5 us (7%)
  local copies, waits for them, and re-layouts  13.7 us (6%)
  other arithmetic  4.87 us (2%)
    unnamed x2, waiting for transfers between devices  48.9 us
    all_to_all x2, waiting for transfers between devices, on_device(): lax.all_to_all(values, 'lane', split_axis=3, concat_axis=1, tiled=True)  25.1 us
    all_to_all x2, blocking collectives, on_device(): lax.all_to_all(moved, 'bank', split_axis=1, concat_axis=2, tiled=True)  24.3 us
    all_to_all x1, blocking collectives, on_device(): lax.all_to_all(moved, 'lane', split_axis=1, concat_axis=3, tiled=True)  16.4 us
    all_to_all x2, waiting for transfers between devices, on_device(): lax.all_to_all(values, 'bank', split_axis=2, concat_axis=1, tiled=True)  16.4 us
    dot_general x16, matrix products, times(): jnp.tensordot(values, table, axes=([dim], [0]), precision=lax.Precision.H...  15.5 us
    all_to_all x1, waiting for transfers between devices, on_device(): lax.all_to_all(moved, 'lane', split_axis=1, concat_axis=3, tiled=True)  11.2 us
    all_to_all x2, starting transfers between devices, on_device(): lax.all_to_all(values, 'bank', split_axis=2, concat_axis=1, tiled=True)  8.69 us
  transfers between devices with their start and end apart: 6, of which 6 were waited for; matrix products, arithmetic and copies ran while one was open for 1% of the time, Pallas kernels for 0%

commit v1 on v0

v1 whole, which is shorter than its diff:
```python
import functools

import jax
import jax.numpy as jnp
from jax import lax
from jax.experimental import pallas as pl
from jax.experimental.pallas import tpu as pltpu
from jax.sharding import PartitionSpec as P

MESH = pl.DeviceIdType.MESH
SIN = (1.0, -1 / 6, 1 / 120, -1 / 5040, 1 / 362880, -1 / 39916800, 1 / 6227020800, -1 / 1307674368000)
COS = (1.0, -1 / 2, 1 / 24, -1 / 720, 1 / 40320, -1 / 3628800, 1 / 479001600, -1 / 87178291200, 1 / 20922789888000)


def series(square, terms):
    total = jnp.full_like(square, terms[-1])
    for term in terms[-2::-1]:
        total = total * square + term
    return total


def sin_cos(turn):
    square = turn * turn
    return turn * series(square, SIN), series(square, COS)


def split(x):
    high = x.astype(jnp.bfloat16)
    return high, (x - high.astype(jnp.float32)).astype(jnp.bfloat16)


def dot3(a, b):
    def one(x, y):
        return lax.dot_general(x, y, (((1,), (0,)), ((), ())), preferred_element_type=jnp.float32)

    return one(a[0], b[0]) + (one(a[1], b[0]) + one(a[0], b[1]))


def turn_table(count, cosine, sine):
    row = lax.broadcasted_iota(jnp.int32, (count, count), 0)
    col = lax.broadcasted_iota(jnp.int32, (count, count), 1)
    apart = row ^ col
    size = jnp.ones((count, count), jnp.float32)
    ones = jnp.zeros((count, count), jnp.int32)
    for place in range(count.bit_length() - 1):
        bit = (apart >> place) & 1
        size = size * jnp.where(bit == 1, sine, cosine)
        ones = ones + bit
    phase = ones & 3
    real = jnp.where(phase == 0, size, jnp.where(phase == 2, -size, 0.0))
    imag = jnp.where(phase == 1, -size, jnp.where(phase == 3, size, 0.0))
    return real, imag


def butterfly(re, im, stride, cosine, sine):
    count, rest = re.shape[0], re.shape[1:]
    parts = (count // (2 * stride), 2, stride) + rest
    re, im = re.reshape(parts), im.reshape(parts)
    ur, vr, ui, vi = re[:, 0], re[:, 1], im[:, 0], im[:, 1]
    new_re = jnp.stack([cosine * ur + sine * vi, cosine * vr + sine * ui], axis=1)
    new_im = jnp.stack([cosine * ui - sine * vr, cosine * vi - sine * ur], axis=1)
    return new_re.reshape((count,) + rest), new_im.reshape((count,) + rest)


def kernel(nb, nl, amp, en, ph, mix, out, marg, tmp, s_a, e_b, b_b, o_b, r_a, cs_b, sn_b, ch, m_in, send, recv):
    n = nb * nl
    depth, rows, lanes = amp.shape[1:]
    per = en.shape[1]
    tiled = per % 8 == 0
    units = rows // per
    piece = rows // nb
    bank, lane = lax.axis_index("bank"), lax.axis_index("lane")
    me = bank * nl + lane

    barrier = pltpu.get_barrier_semaphore()

    def greet(k, carry):
        pl.semaphore_signal(
            barrier, 1, device_id=(lax.rem(bank + k // nl, nb), lax.rem(lane + lax.rem(k, nl), nl)), device_id_type=MESH
        )
        return carry

    lax.fori_loop(1, n, greet, 0)
    pl.semaphore_wait(barrier, n - 1)

    def exchange(src, dst, which):
        def one(k, carry):
            to_bank, to_lane = lax.rem(bank + k // nl, nb), lax.rem(lane + lax.rem(k, nl), nl)
            pltpu.make_async_remote_copy(
                src_ref=src.at[to_bank * nl + to_lane],
                dst_ref=dst.at[me],
                send_sem=send.at[which],
                recv_sem=recv.at[which],
                device_id=(to_bank, to_lane),
                device_id_type=MESH,
            ).start()
            return carry

        lax.fori_loop(1, n, one, 0)
        dst[me] = src[me]

    def arrived(dst, count, sems, which):
        most = dst.at[pl.ds(0, count - 1)]
        pltpu.make_async_copy(most, most, sems.at[which]).wait()

    exchange(en, e_b, 0)

    cosines, sines = jnp.cos(mix[...]), jnp.sin(mix[...])

    def angle(layer, group):
        return cosines[layer : layer + 1, group : group + 1], sines[layer : layer + 1, group : group + 1]

    def local_mix(layer, read, write):
        real, imag = turn_table(lanes, *angle(layer, 0))
        by_lane = split(jnp.concatenate([jnp.concatenate([real, imag], 1), jnp.concatenate([-imag, real], 1)], 0))
        real, imag = turn_table(rows, *angle(layer, 1))
        by_row = split(jnp.concatenate([jnp.concatenate([real, -imag], 1), jnp.concatenate([imag, real], 1)], 0))
        pairs = [read(d) for d in range(depth)]
        stride = 1
        cosine, sine = (jnp.broadcast_to(x, (8, lanes))[None] for x in angle(layer, 2))
        re = jnp.stack([p[0] for p in pairs]).reshape(depth, rows // 8, 8, lanes)
        im = jnp.stack([p[1] for p in pairs]).reshape(depth, rows // 8, 8, lanes)
        while stride < depth:
            re, im = butterfly(re, im, stride, cosine, sine)
            stride *= 2
        re, im = re.reshape(depth, rows, lanes), im.reshape(depth, rows, lanes)
        for d in range(depth):
            both = dot3(split(jnp.concatenate([re[d], im[d]], 1)), by_lane)
            both = dot3(by_row, split(jnp.concatenate([both[:, :lanes], both[:, lanes:]], 0)))
            write(d, both[:rows], both[rows:])

    def first(d):
        if tiled:
            e = en[pl.ds(d * units, units)].reshape(rows, lanes)
        else:
            e = tmp[0, d]
        sine, cosine = sin_cos(ph[0:1] * e)
        return amp[0, d] * cosine + amp[1, d] * sine, amp[1, d] * cosine - amp[0, d] * sine

    def to_units(d, re, im):
        if tiled:
            s_a[pl.ds(d * units, units), 0] = re.reshape(units, per, lanes)
            s_a[pl.ds(d * units, units), 1] = im.reshape(units, per, lanes)
        else:
            tmp[0, d] = re
            tmp[1, d] = im

    if not tiled:
        for d in range(depth):

            def spread(u, carry):
                tmp[0, d, pl.ds(u * per, per)] = en[d * units + u]
                return carry

            lax.fori_loop(0, units, spread, 0)
    local_mix(0, first, to_units)
    if not tiled:
        for d in range(depth):

            def gather(u, carry):
                for part in range(2):
                    s_a[d * units + u, part] = tmp[part, d, pl.ds(u * per, per)]
                return carry

            lax.fori_loop(0, units, gather, 0)

    exchange(s_a, b_b, 1)
    arrived(e_b, n, recv, 0)
    sine, cosine = sin_cos(ph[1:2][None] * e_b[...])
    sn_b[...] = sine
    cs_b[...] = cosine
    arrived(b_b, n, recv, 1)

    step = 8 if tiled else per
    for at in range(0, per, step):
        span = pl.ds(at, step)
        re, im = b_b[:, 0, span], b_b[:, 1, span]
        for layer in range(2):
            stride = 1
            while stride < n:
                cosine, sine = (
                    jnp.broadcast_to(x, (step, lanes))[None, None] for x in angle(layer, 3 if stride < nl else 2)
                )
                re, im = butterfly(re, im, stride, cosine, sine)
                stride *= 2
            if layer == 0:
                cosine, sine = cs_b[:, span], sn_b[:, span]
                re, im = re * cosine + im * sine, im * cosine - re * sine
        o_b[:, 0, span] = re
        o_b[:, 1, span] = im

    exchange(o_b, r_a, 2)
    arrived(r_a, n, recv, 2)

    if not tiled:
        for d in range(depth):

            def place(u, carry):
                for part in range(2):
                    tmp[part, d, pl.ds(u * per, per)] = r_a[d * units + u, part]
                return carry

            lax.fori_loop(0, units, place, 0)

    def second(d):
        if tiled:
            return tuple(r_a[pl.ds(d * units, units), part].reshape(rows, lanes) for part in range(2))
        return tmp[0, d], tmp[1, d]

    def finish(d, re, im):
        out[0, d] = re
        out[1, d] = im
        chance = re * re + im * im
        for g in range(nb):
            ch[g, d] = chance[g * piece : (g + 1) * piece]

    local_mix(1, second, finish)

    def pass_on(k, carry):
        to_bank = lax.rem(bank + k, nb)
        pltpu.make_async_remote_copy(
            src_ref=ch.at[to_bank],
            dst_ref=m_in.at[bank],
            send_sem=send.at[3],
            recv_sem=recv.at[3],
            device_id=(to_bank, lane),
            device_id_type=MESH,
        ).start()
        return carry

    lax.fori_loop(1, nb, pass_on, 0)
    m_in[bank] = ch[bank]
    arrived(m_in, nb, recv, 3)
    total = m_in[0]
    for g in range(1, nb):
        total = total + m_in[g]
    marg[...] = total * (1.0 / nb)
    arrived(e_b, n, send, 0)
    arrived(b_b, n, send, 1)
    arrived(r_a, n, send, 2)
    arrived(m_in, nb, send, 3)


def on_device(nb, nl, amplitudes, energies, phase_angles, mix_angles):
    _, depth, rows, lanes = amplitudes.shape
    n = nb * nl
    per = depth * rows // n
    piece = rows // nb
    f32 = jnp.float32
    state = pltpu.VMEM((n, 2, per, lanes), f32)
    level = pltpu.VMEM((n, per, lanes), f32)
    vmem = pl.BlockSpec(memory_space=pltpu.VMEM)
    return pl.pallas_call(
        functools.partial(kernel, nb, nl),
        name="register",
        out_shape=(
            jax.ShapeDtypeStruct(amplitudes.shape, f32),
            jax.ShapeDtypeStruct((depth, piece, lanes), f32),
        ),
        in_specs=[vmem] * 4,
        out_specs=(vmem, vmem),
        scratch_shapes=[
            pltpu.VMEM((2, depth, rows, lanes) if per % 8 else (1, 1, 8, 128), f32),
            state,
            level,
            state,
            state,
            state,
            level,
            level,
            pltpu.VMEM((nb, depth, piece, lanes), f32),
            pltpu.VMEM((nb, depth, piece, lanes), f32),
            pltpu.SemaphoreType.DMA((4,)),
            pltpu.SemaphoreType.DMA((4,)),
        ],
        compiler_params=pltpu.CompilerParams(collective_id=0, has_side_effects=True),
    )(amplitudes, energies.reshape(n, per, lanes), phase_angles, mix_angles)


def solution(mesh):
    placed = (P(None, ("bank", "lane"), None, None), P(("bank", "lane"), None, None), P(), P())
    return jax.shard_map(
        functools.partial(on_device, mesh.shape["bank"], mesh.shape["lane"]),
        mesh=mesh,
        in_specs=placed,
        out_specs=(P(None, ("bank", "lane"), None, None), P("lane", "bank", None)),
        check_vma=False,
    )
```

time: 225 us -> 51.8 us (0.23)
  waiting for transfers between devices: 102 us -> 0 us
  Pallas kernels: 0 us -> 48.5 us
  blocking collectives: 40.7 us -> 0 us
  between operations: 26.5 us -> 0.65 us
  starting transfers between devices: 20.7 us -> 0 us
  matrix products: 15.5 us -> 0 us
  local copies, waits for them, and re-layouts: 13.7 us -> 2.5 us
  other arithmetic: 4.87 us -> 0 us
    all_to_all x5 -> x0, waiting for transfers between devices: 52.7 us -> none  [the longest x2 25.1 us: on_device(): lax.all_to_all(values, 'lane', split_axis=3, concat_axis=1, tiled=True)]
    unnamed x2 -> x0, waiting for transfers between devices: 48.9 us -> none
    pallas_call x0 -> x1, Pallas kernels: none -> 48.5 us  [on_device(): pl.pallas_call(functools.partial(kernel, nb, nl), name='register', out_sh...]
    all_to_all x3 -> x0, blocking collectives: 40.7 us -> none  [the longest x2 24.3 us: on_device(): lax.all_to_all(moved, 'bank', split_axis=1, concat_axis=2, tiled=True)]
    all_to_all x5 -> x0, starting transfers between devices: 20.7 us -> none  [the longest x2 8.69 us: on_device(): lax.all_to_all(values, 'bank', split_axis=2, concat_axis=1, tiled=True)]
    dot_general x16 -> x0, matrix products: 15.5 us -> none  [times(): jnp.tensordot(values, table, axes=([dim], [0]), precision=lax.Precision.H...]
    another operation x6 -> x0, local copies, waits for them, and re-layouts: 3.48 us -> none  [apply_along(): return jnp.stack([by_real[0] - by_imag[1], by_real[1] + by_imag[0]])]
    another operation x8 -> x0, other arithmetic: 3.27 us -> none  [the longest x2 3.05 us: diagonal_step(): jnp.stack([values[0] * jnp.cos(turn) + values[1] * jnp.sin(turn), values[...]
  transfers between devices with their start and end apart: 6 -> 0, of which waited for: 6 -> 0; matrix products, arithmetic and copies ran while one was open for 1% -> 0% of each run, Pallas kernels for 0% -> 0%
where the time goes in v1:
time: 51.8 us; the launch traced here: 51.7 us
  Pallas kernels  48.5 us (94%)
  local copies, waits for them, and re-layouts  2.5 us (5%)
  between operations  0.65 us (1%)
    pallas_call x1, Pallas kernels, on_device(): pl.pallas_call(functools.partial(kernel, nb, nl), name='register', out_sh...  48.5 us
    unnamed x4, local copies, waits for them, and re-layouts  2.5 us

profile of v1, /device:TPU:0, one launch (start us, length us, event | category | flops | bytes accessed | tf_op | source)
XLA Modules:
  0.0 51.7 jit_solution(14114808304337936849)
XLA Ops:
  0.6 48.5 %register.1 = (f32[2,4,128,128]{3,2,1,0:T(8,128)}, f32[4,16,128]{2,1,0:T(8,128)}) custom-call(f32[2,4,128,128]{3,2,1,0:T(8,128)} %amp.1, f32[32,16,128]{2,1,0:T(8,128)} %bitcast.1, f32[2,128]{1,0:T(2,128)} %ph.1, f32[2,4]{1,0:T(2,128)} %mix.1), custom_call_target="tpu_custom_call" | custom-call | tf_op jit(solution)/shard_map/register/pallas_call | solution.py:253
  49.2 0.0 copy-start
  49.2 1.9 %copy.8 = f32[2,4,128,128]{3,2,1,0:T(8,128)} copy(f32[2,4,128,128]{3,2,1,0:T(8,128)} %get-tuple-element.4) | data formatting | bytes 1048576
  51.1 0.0 copy-done
  51.1 0.6 %copy.9 = f32[4,16,128]{2,1,0:T(8,128)} copy(f32[4,16,128]{2,1,0:T(8,128)S(1)} %copy-done) | data formatting | bytes 65536
Async XLA Ops:
  49.2 1.9 %copy-start = (f32[4,16,128]{2,1,0:T(8,128)S(1)}, f32[4,16,128]{2,1,0:T(8,128)}, u32[]{:S(2)}) copy-start(f32[4,16,128]{2,1,0:T(8,128)} %get-tuple-element.5) | copy-start | bytes 98308

commit v2 on v1

v2 whole, which is shorter than its diff:
```python
import functools

import jax
import jax.numpy as jnp
from jax import lax
from jax.experimental import pallas as pl
from jax.experimental.pallas import tpu as pltpu
from jax.sharding import PartitionSpec as P

MESH = pl.DeviceIdType.MESH
SIN = (1.0, -1 / 6, 1 / 120, -1 / 5040, 1 / 362880, -1 / 39916800, 1 / 6227020800, -1 / 1307674368000)
COS = (1.0, -1 / 2, 1 / 24, -1 / 720, 1 / 40320, -1 / 3628800, 1 / 479001600, -1 / 87178291200, 1 / 20922789888000)


def series(square, terms):
    total = jnp.full_like(square, terms[-1])
    for term in terms[-2::-1]:
        total = total * square + term
    return total


def sin_cos(turn):
    square = turn * turn
    return turn * series(square, SIN), series(square, COS)


def split(x):
    high = x.astype(jnp.bfloat16)
    return high, (x - high.astype(jnp.float32)).astype(jnp.bfloat16)


def dot3(a, b):
    def one(x, y):
        return lax.dot_general(x, y, (((1,), (0,)), ((), ())), preferred_element_type=jnp.float32)

    return one(a[0], b[0]) + (one(a[1], b[0]) + one(a[0], b[1]))


def turn_table(count, cosine, sine):
    row = lax.broadcasted_iota(jnp.int32, (count, count), 0)
    col = lax.broadcasted_iota(jnp.int32, (count, count), 1)
    apart = row ^ col
    size = jnp.ones((count, count), jnp.float32)
    ones = jnp.zeros((count, count), jnp.int32)
    for place in range(count.bit_length() - 1):
        bit = (apart >> place) & 1
        size = size * jnp.where(bit == 1, sine, cosine)
        ones = ones + bit
    phase = ones & 3
    real = jnp.where(phase == 0, size, jnp.where(phase == 2, -size, 0.0))
    imag = jnp.where(phase == 1, -size, jnp.where(phase == 3, size, 0.0))
    return real, imag


def butterfly(re, im, stride, cosine, sine):
    count, rest = re.shape[0], re.shape[1:]
    parts = (count // (2 * stride), 2, stride) + rest
    re, im = re.reshape(parts), im.reshape(parts)
    ur, vr, ui, vi = re[:, 0], re[:, 1], im[:, 0], im[:, 1]
    new_re = jnp.stack([cosine * ur + sine * vi, cosine * vr + sine * ui], axis=1)
    new_im = jnp.stack([cosine * ui - sine * vr, cosine * vi - sine * ur], axis=1)
    return new_re.reshape((count,) + rest), new_im.reshape((count,) + rest)


def kernel(
    nb, nl, halves, amp_hbm, en_hbm, ph, mix, out, marg,
    amp, en, tmp, s_a, e_b, b_b, o_b, r_a, cs_b, sn_b, part_done, ch, m_in, load, send, recv,
):
    n = nb * nl
    depth, rows, lanes = amp.shape[1:]
    per = en.shape[1]
    step = per // halves
    tiled = per % 8 == 0
    units = rows // per
    piece = rows // nb
    last = 2 * halves + 1
    bank, lane = lax.axis_index("bank"), lax.axis_index("lane")
    me = bank * nl + lane

    load_en = pltpu.make_async_copy(en_hbm, en, load.at[0])
    load_amp = pltpu.make_async_copy(amp_hbm, amp, load.at[1])
    load_en.start()
    load_amp.start()
    barrier = pltpu.get_barrier_semaphore()

    def partner(k):
        return lax.rem(bank + lax.rem(k, nb), nb), lax.rem(lane + k // nb, nl)

    def greet(k, carry):
        pl.semaphore_signal(barrier, 1, device_id=partner(k), device_id_type=MESH)
        return carry

    lax.fori_loop(1, n, greet, 0)

    def exchange(src, dst, which):
        def one(k, carry):
            to_bank, to_lane = partner(k)
            pltpu.make_async_remote_copy(
                src_ref=src.at[to_bank * nl + to_lane],
                dst_ref=dst.at[me],
                send_sem=send.at[which],
                recv_sem=recv.at[which],
                device_id=(to_bank, to_lane),
                device_id_type=MESH,
            ).start()
            return carry

        lax.fori_loop(1, n, one, 0)
        dst[me] = src[me]

    def arrived(dst, count, sems, which):
        most = dst.at[pl.ds(0, count - 1)]
        pltpu.make_async_copy(most, most, sems.at[which]).wait()

    cosines, sines = jnp.cos(mix[...]), jnp.sin(mix[...])

    def angle(layer, group):
        return cosines[layer : layer + 1, group : group + 1], sines[layer : layer + 1, group : group + 1]

    def tables(layer, count):
        real, imag = turn_table(lanes, *angle(layer, 0))
        by_lane = split(jnp.concatenate([jnp.concatenate([real, imag], 1), jnp.concatenate([-imag, real], 1)], 0))
        real, imag = turn_table(count, *angle(layer, 1))
        by_row = split(jnp.concatenate([jnp.concatenate([real, -imag], 1), jnp.concatenate([imag, real], 1)], 0))
        return by_lane, by_row

    def local_mix(layer, by_lane, by_row, count, read, write):
        pairs = [read(d) for d in range(depth)]
        stride = 1
        cosine, sine = (jnp.broadcast_to(x, (8, lanes))[None] for x in angle(layer, 2))
        re = jnp.stack([p[0] for p in pairs]).reshape(depth, count // 8, 8, lanes)
        im = jnp.stack([p[1] for p in pairs]).reshape(depth, count // 8, 8, lanes)
        while stride < depth:
            re, im = butterfly(re, im, stride, cosine, sine)
            stride *= 2
        re, im = re.reshape(depth, count, lanes), im.reshape(depth, count, lanes)
        for d in range(depth):
            both = dot3(split(jnp.concatenate([re[d], im[d]], 1)), by_lane)
            both = dot3(by_row, split(jnp.concatenate([both[:, :lanes], both[:, lanes:]], 0)))
            write(d, both[:count], both[count:])

    first_tables = tables(0, rows)
    second_tables = tables(1, rows // halves)

    load_en.wait()
    pl.semaphore_wait(barrier, n - 1)
    exchange(en, e_b, 0)
    load_amp.wait()

    def first(d):
        if tiled:
            e = en[pl.ds(d * units, units)].reshape(rows, lanes)
        else:
            e = tmp[0, d]
        sine, cosine = sin_cos(ph[0:1] * e)
        return amp[0, d] * cosine + amp[1, d] * sine, amp[1, d] * cosine - amp[0, d] * sine

    def to_units(d, re, im):
        if tiled:
            for part, x in enumerate((re, im)):
                x = x.reshape(units, halves, step, lanes)
                for h in range(halves):
                    s_a[h, pl.ds(d * units, units), part] = x[:, h]
        else:
            tmp[0, d] = re
            tmp[1, d] = im

    if not tiled:
        for d in range(depth):

            def spread(u, carry):
                tmp[0, d, pl.ds(u * per, per)] = en[d * units + u]
                return carry

            lax.fori_loop(0, units, spread, 0)
    local_mix(0, *first_tables, rows, first, to_units)
    if not tiled:
        for d in range(depth):

            def gather(u, carry):
                for part in range(2):
                    s_a[0, d * units + u, part] = tmp[part, d, pl.ds(u * per, per)]
                return carry

            lax.fori_loop(0, units, gather, 0)

    for h in range(halves):
        exchange(s_a.at[h], b_b.at[h], 1 + h)
    arrived(e_b, n, recv, 0)
    sine, cosine = sin_cos(ph[1:2][None] * e_b[...])
    sn_b[...] = sine
    cs_b[...] = cosine

    for h in range(halves):
        arrived(b_b.at[h], n, recv, 1 + h)
        span = pl.ds(h * step, step)
        re, im = b_b[h, :, 0], b_b[h, :, 1]
        for layer in range(2):
            stride = 1
            while stride < n:
                cosine, sine = (
                    jnp.broadcast_to(x, (step, lanes))[None, None] for x in angle(layer, 3 if stride < nl else 2)
                )
                re, im = butterfly(re, im, stride, cosine, sine)
                stride *= 2
            if layer == 0:
                cosine, sine = cs_b[:, span], sn_b[:, span]
                re, im = re * cosine + im * sine, im * cosine - re * sine
        o_b[h, :, 0] = re
        o_b[h, :, 1] = im
        exchange(o_b.at[h], r_a.at[h], 1 + halves + h)

    def second(h, d):
        if tiled:
            return tuple(
                r_a[h, pl.ds(d * units, units), part].reshape(rows // halves, lanes) for part in range(2)
            )
        return tmp[0, d], tmp[1, d]

    def keep(d, re, im):
        part_done[0, d] = re
        part_done[1, d] = im

    def pass_on(d):
        def one(k, carry):
            to_bank = lax.rem(bank + k, nb)
            pltpu.make_async_remote_copy(
                src_ref=ch.at[d, to_bank],
                dst_ref=m_in.at[bank, d],
                send_sem=send.at[last],
                recv_sem=recv.at[last],
                device_id=(to_bank, lane),
                device_id_type=MESH,
            ).start()
            return carry

        lax.fori_loop(1, nb, one, 0)
        m_in[bank, d] = ch[d, bank]

    def finish(d, re, im):
        if halves == 2:
            cosine, sine = angle(1, 1)
            ur, ui, vr, vi = part_done[0, d], part_done[1, d], re, im
            shape = (units, 1, step, lanes)
            re = [cosine * ur + sine * vi, cosine * vr + sine * ui]
            im = [cosine * ui - sine * vr, cosine * vi - sine * ur]
            re = jnp.concatenate([x.reshape(shape) for x in re], 1).reshape(rows, lanes)
            im = jnp.concatenate([x.reshape(shape) for x in im], 1).reshape(rows, lanes)
        chance = re * re + im * im
        for g in range(nb):
            ch[d, g] = chance[g * piece : (g + 1) * piece]
        out[0, d] = re
        out[1, d] = im
        pass_on(d)

    for h in range(halves):
        arrived(r_a.at[h], n, recv, 1 + halves + h)
        if not tiled:
            for d in range(depth):

                def place(u, carry):
                    for part in range(2):
                        tmp[part, d, pl.ds(u * per, per)] = r_a[h, d * units + u, part]
                    return carry

                lax.fori_loop(0, units, place, 0)
        write = finish if h == halves - 1 else keep
        local_mix(1, *second_tables, rows // halves, functools.partial(second, h), write)

    arrived(m_in, nb, recv, last)
    total = m_in[0]
    for g in range(1, nb):
        total = total + m_in[g]
    marg[...] = total * (1.0 / nb)
    arrived(e_b, n, send, 0)
    for h in range(halves):
        arrived(b_b.at[h], n, send, 1 + h)
        arrived(r_a.at[h], n, send, 1 + halves + h)
    arrived(m_in, nb, send, last)


def on_device(nb, nl, amplitudes, energies, phase_angles, mix_angles):
    _, depth, rows, lanes = amplitudes.shape
    n = nb * nl
    per = depth * rows // n
    halves = 2 if per % 16 == 0 else 1
    piece = rows // nb
    f32 = jnp.float32
    state = pltpu.VMEM((halves, n, 2, per // halves, lanes), f32)
    level = pltpu.VMEM((n, per, lanes), f32)
    vmem = pl.BlockSpec(memory_space=pltpu.VMEM)
    anywhere = pl.BlockSpec(memory_space=pl.ANY)
    whole = pltpu.VMEM((2, depth, rows, lanes), f32)
    return pl.pallas_call(
        functools.partial(kernel, nb, nl, halves),
        name="register",
        out_shape=(pltpu.VMEM(amplitudes.shape, f32), pltpu.VMEM((depth, piece, lanes), f32)),
        in_specs=[anywhere, anywhere, vmem, vmem],
        out_specs=(vmem, vmem),
        scratch_shapes=[
            whole,
            level,
            whole if per % 8 else pltpu.VMEM((1, 1, 8, 128), f32),
            state,
            level,
            state,
            state,
            state,
            level,
            level,
            pltpu.VMEM((2, depth, rows // halves, lanes), f32),
            pltpu.VMEM((depth, nb, piece, lanes), f32),
            pltpu.VMEM((nb, depth, piece, lanes), f32),
            pltpu.SemaphoreType.DMA((2,)),
            pltpu.SemaphoreType.DMA((2 * halves + 2,)),
            pltpu.SemaphoreType.DMA((2 * halves + 2,)),
        ],
        compiler_params=pltpu.CompilerParams(collective_id=0, has_side_effects=True),
    )(amplitudes, energies.reshape(n, per, lanes), phase_angles, mix_angles)


def solution(mesh):
    placed = (P(None, ("bank", "lane"), None, None), P(("bank", "lane"), None, None), P(), P())
    return jax.shard_map(
        functools.partial(on_device, mesh.shape["bank"], mesh.shape["lane"]),
        mesh=mesh,
        in_specs=placed,
        out_specs=(P(None, ("bank", "lane"), None, None), P("lane", "bank", None)),
        check_vma=False,
    )
```

time: 51.8 us -> 44.6 us (0.86)
  Pallas kernels: 48.5 us -> 42.4 us
  local copies, waits for them, and re-layouts: 2.5 us -> 1.41 us
    pallas_call x1, Pallas kernels: 48.5 us -> 42.4 us  [on_device(): pl.pallas_call(functools.partial(kernel, nb, nl, halves), name='register'...]
    unnamed x4 -> x2, local copies, waits for them, and re-layouts: 2.5 us -> 1.41 us
where the time goes in v2:
time: 44.6 us; the launch traced here: 44.5 us
  Pallas kernels  42.4 us (95%)
  local copies, waits for them, and re-layouts  1.41 us (3%)
  between operations  0.64 us (1%)
    pallas_call x1, Pallas kernels, on_device(): pl.pallas_call(functools.partial(kernel, nb, nl, halves), name='register'...  42.4 us
    unnamed x2, local copies, waits for them, and re-layouts  1.41 us

profile of v2, /device:TPU:0, one launch (start us, length us, event | category | flops | bytes accessed | tf_op | source)
XLA Modules:
  0.0 44.5 jit_solution(10109937915535827731)
XLA Ops:
  0.6 42.4 %register.1 = (f32[2,4,128,128]{3,2,1,0:T(8,128)S(1)}, f32[4,16,128]{2,1,0:T(8,128)S(1)}) custom-call(f32[2,4,128,128]{3,2,1,0:T(8,128)} %amp_hbm.1, f32[32,16,128]{2,1,0:T(8,128)} %bitcast.1, f32[2,128]{1,0:T(2,128)} %ph.1, f32[2,4]{1,0:T(2,128)} %mix.1), custom_call_target="tpu_custom_call" | custom-call | tf_op jit(solution)/shard_map/register/pallas_call | solution.py:294
  43.0 0.8 %copy.8 = f32[2,4,128,128]{3,2,1,0:T(8,128)} copy(f32[2,4,128,128]{3,2,1,0:T(8,128)S(1)} %get-tuple-element.2) | data formatting | bytes 1048576
  43.8 0.6 %copy.9 = f32[4,16,128]{2,1,0:T(8,128)} copy(f32[4,16,128]{2,1,0:T(8,128)S(1)} %get-tuple-element.3) | data formatting | bytes 65536

commit v3 on v2

--- a/solution.py
+++ b/solution.py
@@ -84,7 +84,7 @@
     barrier = pltpu.get_barrier_semaphore()
 
     def partner(k):
-        return lax.rem(bank + lax.rem(k, nb), nb), lax.rem(lane + k // nb, nl)
+        return lax.rem(bank + nb - lax.rem(k, nb), nb), lax.rem(lane + k // nb, nl)
 
     def greet(k, carry):
         pl.semaphore_signal(barrier, 1, device_id=partner(k), device_id_type=MESH)

time: 44.6 us -> 43.6 us (0.978)
  Pallas kernels: 42.4 us -> 41.4 us
    pallas_call x1, Pallas kernels: 42.4 us -> 41.4 us  [on_device(): pl.pallas_call(functools.partial(kernel, nb, nl, halves), name='register'...]
where the time goes in v3:
time: 43.6 us; the launch traced here: 43.4 us
  Pallas kernels  41.4 us (95%)
  local copies, waits for them, and re-layouts  1.41 us (3%)
  between operations  0.64 us (1%)
    pallas_call x1, Pallas kernels, on_device(): pl.pallas_call(functools.partial(kernel, nb, nl, halves), name='register'...  41.4 us
    unnamed x2, local copies, waits for them, and re-layouts  1.41 us

profile of v3, /device:TPU:0, one launch (start us, length us, event | category | flops | bytes accessed | tf_op | source)
XLA Modules:
  0.0 43.4 jit_solution(639378012425648927)
XLA Ops:
  0.6 41.4 %register.1 = (f32[2,4,128,128]{3,2,1,0:T(8,128)S(1)}, f32[4,16,128]{2,1,0:T(8,128)S(1)}) custom-call(f32[2,4,128,128]{3,2,1,0:T(8,128)} %amp_hbm.1, f32[32,16,128]{2,1,0:T(8,128)} %bitcast.1, f32[2,128]{1,0:T(2,128)} %ph.1, f32[2,4]{1,0:T(2,128)} %mix.1), custom_call_target="tpu_custom_call" | custom-call | tf_op jit(solution)/shard_map/register/pallas_call | solution.py:294
  42.0 0.8 %copy.8 = f32[2,4,128,128]{3,2,1,0:T(8,128)} copy(f32[2,4,128,128]{3,2,1,0:T(8,128)S(1)} %get-tuple-element.2) | data formatting | bytes 1048576
  42.8 0.6 %copy.9 = f32[4,16,128]{2,1,0:T(8,128)} copy(f32[4,16,128]{2,1,0:T(8,128)S(1)} %get-tuple-element.3) | data formatting | bytes 65536
